TPU v7x, 128 devices: a 2x2x16 block of a 8x8x16 slice. The times are simulated.
128 devices in a mesh: groups: 4 (over x, y), blk: 32 (over z, core).
Axes of the slice: x: 2, y: 2, z: 16, core: 2. Of those that a mesh axis runs over, the one named last changes fastest.
The devices are a block of a 8x8x16 slice.
Arguments:
- points: bfloat16 [196608, 1024], P(('groups', 'blk')), parts along dimension 0, may hold values from -6 to 6
- coverage: float32 [196608], P(('groups', 'blk')), parts along dimension 0, may hold values from 0 to 1.5
- candidates: bfloat16 [16384, 1024], P(('groups', 'blk')), parts along dimension 0, may hold values from -6 to 6
- cand_count: int32 [128], P(('groups', 'blk')), parts along dimension 0, may hold values from 16 to 128, as said below
- acc_index: int32 [128, 16], P(('groups', 'blk')), parts along dimension 0, may hold values from 0 to 127, as said below
Outputs:
- gain_out: float32 [16384], P(('groups', 'blk')), parts along dimension 0
- new_coverage: float32 [196608], P(('groups', 'blk')), parts along dimension 0
There are 4 independent parts, one for each index of `groups`. A program takes and returns all parts, laid end to end along the dimension named above; each array names one. Nothing has to cross between parts.
Inputs may be any that keep to these rules, and one draw needn't show every extreme that they name: `cand_count`: some device has all 128 slots live. `acc_index`: each entry of row b is below cand_count[b]; entries may repeat.
All inputs are finite; a program needn't handle non-finite values.
Results may differ from a plain program's by a relative error of at most 0.0003.
Values may be sent and summed in bfloat16 or wider, within the bound.
A program may use at most 64 MiB of HBM per device.

v0:
```python
import jax
import jax.numpy as jnp
from jax import lax
from jax.sharding import Mesh
from jax.sharding import PartitionSpec as P

BLK = ("blk_0", "blk_1")
GROUPS_BLK = ("groups", "blk_0", "blk_1")


def in_blocks(shard, dim, count):
    dims = shard.shape
    parts = shard.reshape(*dims[:dim], count, dims[dim] // count, *dims[dim + 1 :])
    return jnp.moveaxis(parts, dim, 0)


def summed_on_arrival(shard, axis, dim):
    parts = in_blocks(shard, dim, lax.axis_size(axis))
    arrived = lax.all_to_all(parts, axis, split_axis=0, concat_axis=0, tiled=True)
    return arrived.sum(axis=0)


def gathered_by_axis(shard, axes, dim):
    if not axes:
        return shard
    nearer = lax.all_gather(shard, axes[-1], axis=dim, tiled=True)
    return gathered_by_axis(nearer, axes[:-1], dim)


def block_terms(points, coverage, cand_block, factor):
    similar = (
        jnp.einsum("pd,cd->pc", points, cand_block, preferred_element_type=jnp.float32) * factor
    )
    return (similar, jnp.sum(jnp.maximum(similar - coverage[:, None], 0.0), axis=0))


def per_device(points, coverage, candidates, cand_count, acc_index):
    width = points.shape[1]
    slots = candidates.shape[0]
    factor = 1.0 / jnp.sqrt(jnp.float32(width))
    devices = lax.axis_size(BLK)
    point_total = jnp.float32(points.shape[0] * devices)
    slot_ids = jnp.arange(slots, dtype=jnp.int32)
    cover = coverage
    shard_rows = lax.all_gather(candidates, BLK, axis=0, tiled=True)
    similar, sums = block_terms(points, coverage, shard_rows, factor)
    every_sum = sums
    every_sum, cover = (every_sum, cover)
    gain_sum = summed_on_arrival(every_sum, BLK, 0)
    live_rows = slot_ids < cand_count[0]
    gain_out = jnp.where(live_rows, gain_sum / point_total, 0.0)
    picked = jnp.take(candidates, acc_index[0], axis=0)
    similar = (
        jnp.einsum(
            "pd,ad->pa",
            points,
            gathered_by_axis(picked, ("blk_1", "blk_0"), 0),
            preferred_element_type=jnp.float32,
        )
        * factor
    )
    new_coverage = jnp.maximum(coverage, jnp.max(similar, axis=1))
    return (gain_out, new_coverage)


def solution(mesh):
    split = Mesh(mesh.devices.reshape(mesh.shape["groups"], 16, 2), ("groups", "blk_0", "blk_1"))
    return jax.shard_map(
        per_device,
        mesh=split,
        in_specs=(
            P(GROUPS_BLK, None),
            P(GROUPS_BLK),
            P(GROUPS_BLK, None),
            P(GROUPS_BLK),
            P(GROUPS_BLK, None),
        ),
        out_specs=(P(GROUPS_BLK), P(GROUPS_BLK)),
        check_vma=False,
    )
```

profile of v0, /device:TPU:69, one launch (start us, length us, event | category | flops | bytes accessed | tf_op | source)
XLA Modules:
  0.0 137.2 jit_solution(8278887492679083085)
XLA Ops:
  7.2 0.0 copy-start
  7.2 0.1 all-gather.3.cloned.1.call-start
  7.3 0.7 all-gather.3.cloned.1.call-update
  8.0 0.1 all-gather.5.cloned.1.call-start
  8.1 0.7 fusion.1
  8.8 1.6 %gather_fusion = bf16[16,1024]{1,0:T(8,128)(2,1)S(1)} fusion(bf16[128,1024]{1,0:T(8,128)(2,1)} %param.7, s32[1024]{0:T(1024)S(1)} %pad_clamp_fusion), kind=kCustom, calls=%fused_computation | custom fusion | bytes 65600 | tf_op jit(solution)/shard_map/jit(_take)/gather | solution.py:52
  10.4 0.7 compare_and_fusion
  11.1 0.1 broadcast_select_fusion
  11.1 41.2 %all_gather.10 = bf16[256,1024]{1,0:T(8,128)(2,1)} all-gather(bf16[16,1024]{1,0:T(8,128)(2,1)S(1)} %broadcast_select_fusion), channel_id=1, replica_groups=mesh['groups'=4,'blk_0'=16,'blk_1'=2] {'blk_0'}, dimensions={0}, use_global_device_ids=true | all-gather | bytes 557056 | tf_op jit(solution)/shard_map/all_gather | solution.py:26
  52.4 0.1 all-gather.5.cloned.1.call-update
  53.1 40.9 %all-gather.3.cloned.1.call-done = bf16[4096,1024]{1,0:T(8,128)(2,1)} async-done(((bf16[128,1024]{1,0:T(8,128)(2,1)}), bf16[4096,1024]{1,0:T(8,128)(2,1)}) %all-gather.3.cloned.1.call-update) | async-done | bytes 8388624 | tf_op jit(solution)/shard_map/all_gather | solution.py:45
  94.0 0.0 copy-done
  94.0 17.1 %maximum_reduce_fusion = f32[4096]{0:T(1024)} fusion(bf16[1536,1024]{1,0:T(8,128)(2,1)S(1)} %copy-done, bf16[4096,1024]{1,0:T(8,128)(2,1)} %all-gather.3.cloned.1.call-done, f32[1536]{0:T(1024)} %param.6), kind=kOutput, calls=%fused_computation.1 | convolution fusion | flops 12910063616 | bytes 11556864 | tf_op jit(solution)/shard_map/pd,cd->pc/dot_general | solution.py:32
  111.1 0.0 copy-start.1
  111.1 7.2 %all-to-all-start = ((f32[32,1,128]{2,1,0:T(1,128)}), f32[32,1,128]{2,1,0:T(1,128)S(1)}, u32[]{:S(2)}, u32[]{:S(2)}) async-start(f32[32,1,128]{2,1,0:T(1,128)} %bitcast.1), calls=%async_computation | async-start | bytes 32768 | tf_op jit(solution)/shard_map/all_to_all | solution.py:19
  118.2 0.0 all-gather.5.cloned.1.call-done
  118.3 3.1 %fusion = f32[1536]{0:T(1024)S(1)} fusion(bf16[512,1024]{1,0:T(8,128)(2,1)} %all-gather.5.cloned.1.call-done, bf16[1536,1024]{1,0:T(8,128)(2,1)S(1)} %copy-done), kind=kOutput, calls=%fused_computation.3 | convolution fusion | flops 1612184064 | bytes 4200448 | tf_op jit(solution)/shard_map/pd,ad->pa/dot_general | solution.py:54
  121.3 0.0 copy-done.1
  121.4 0.6 max.11
  122.0 7.9 %all-to-all-done = f32[32,1,128]{2,1,0:T(1,128)S(1)} async-done(((f32[32,1,128]{2,1,0:T(1,128)}), f32[32,1,128]{2,1,0:T(1,128)S(1)}, u32[]{:S(2)}, u32[]{:S(2)}) %all-to-all-start) | async-done | bytes 16416 | tf_op jit(solution)/shard_map/all_to_all | solution.py:19
  129.8 0.5 compare_select_fusion.2
  (2 shorter events, 0.0 us)
Async XLA Ops:
  7.2 86.8 %copy-start = (bf16[1536,1024]{1,0:T(8,128)(2,1)S(1)}, bf16[1536,1024]{1,0:T(8,128)(2,1)}, u32[]{:S(2)}) copy-start(bf16[1536,1024]{1,0:T(8,128)(2,1)} %param.5) | copy-start | bytes 9437188
  7.2 86.8 %all-gather.3.cloned.1.call-start = ((), (), s32[]{:S(2)}) async-start(), calls=%async_computation.1 | async-start | bytes 8650752 | tf_op jit(solution)/shard_map/all_gather | solution.py:45
  8.0 110.3 %all-gather.5.cloned.1.call-start = ((), (), s32[]{:S(2)}) async-start(), calls=%async_computation.2 | async-start | bytes 1572864 | tf_op jit(solution)/shard_map/all_gather | solution.py:26
  111.1 10.3 %copy-start.1 = (f32[1536]{0:T(1024)S(1)}, f32[1536]{0:T(1024)}, u32[]{:S(2)}) copy-start(f32[1536]{0:T(1024)} %param.6) | copy-start | bytes 18436
  111.1 18.7 %all-to-all-start = ((f32[32,1,128]{2,1,0:T(1,128)}), f32[32,1,128]{2,1,0:T(1,128)S(1)}, u32[]{:S(2)}, u32[]{:S(2)}) async-start(f32[32,1,128]{2,1,0:T(1,128)} %bitcast.1), calls=%async_computation | async-start | bytes 32768 | tf_op jit(solution)/shard_map/all_to_all | solution.py:19
Sparse Core Ops, SparseCore 0:
  9.7 84.1 all-gather.2
  95.6 12.3 all-gather.4
where the time goes:
time: 138 us; the launch traced here: 137 us
  waiting for transfers between devices  49.5 us (36%)
  blocking collectives  41.2 us (30%)
  matrix products  20.2 us (15%)
  between operations  14.8 us (11%)
  starting transfers between devices  7.28 us (5%)
  other arithmetic  2.62 us (2%)
  local copies, waits for them, and re-layouts  1.61 us (1%)
    all_gather x1, blocking collectives, gathered_by_axis(): nearer = lax.all_gather(shard, axes[-1], axis=dim, tiled=True)  41.2 us
    all_gather x1, waiting for transfers between devices, per_device(): shard_rows = lax.all_gather(candidates, BLK, axis=0, tiled=True)  40.9 us
    dot_general x1, matrix products, block_terms(): jnp.einsum('pd,cd->pc', points, cand_block, preferred_element_type=jnp.fl...  17.1 us
    all_to_all x1, waiting for transfers between devices, summed_on_arrival(): lax.all_to_all(parts, axis, split_axis=0, concat_axis=0, tiled=True)  7.85 us
    all_to_all x1, starting transfers between devices, summed_on_arrival(): lax.all_to_all(parts, axis, split_axis=0, concat_axis=0, tiled=True)  7.16 us
    dot_general x1, matrix products, per_device(): jnp.einsum('pd,ad->pa', points, gathered_by_axis(picked, ('blk_1', 'blk_0...  3.06 us
  transfers between devices with their start and end apart: 3, of which 2 were waited for; matrix products, arithmetic and copies ran while one was open for 17% of the time, Pallas kernels for 0%

commit v1 on v0

v1 whole, which is shorter than its diff:
```python
import functools

import jax
import jax.numpy as jnp
from jax import lax
from jax.experimental import pallas as pl
from jax.experimental.pallas import tpu as pltpu
from jax.sharding import PartitionSpec as P

GROUPS_BLK = ("groups", "blk")
CORES = 2
LANES = 128
CHUNK = 32
TILE = 256
DEAD = -3.0e38


def kernel(
    chips, total_points, count_ref, acc_ref, points_hbm, cover_ref, cands_hbm,
    gain_ref, newcov_ref,
    pts, rows, covb, best, marks, gacc, sums, inbox,
    load_sem, send_sem, recv_sem, push_sem, land_sem, mark_send, mark_recv, mark_push, mark_land,
    sum_send, sum_recv,
):
    npts, width = pts.shape
    slots = cands_hbm.shape[0]
    chip_rows = CORES * slots
    per_block = slots // CHUNK
    half = per_block // 2
    far = chips // 2
    steps = (far - 1) * per_block + half
    tiles = npts // TILE
    scale = jnp.sqrt(jnp.float32(width))
    factor = 1.0 / scale

    me = lax.axis_index("blk")
    z, core = me // CORES, me % CORES
    up = ((z + 1) % chips) * CORES + core
    down = ((z + chips - 1) % chips) * CORES + core
    partner = z * CORES + (1 - core)

    own = pltpu.make_async_copy(
        cands_hbm, rows.at[pl.ds(pl.multiple_of(core * slots, slots), slots)], load_sem.at[0]
    )
    own.start()
    resident = pltpu.make_async_copy(points_hbm, pts, load_sem.at[1])
    resident.start()

    lane = lax.broadcasted_iota(jnp.int32, (1, LANES), 1)
    mark = jnp.full((1, LANES), DEAD, jnp.float32)
    for a in range(acc_ref.shape[1]):
        mark = jnp.where(lane == acc_ref[0, a], 0.0, mark)
    marks[core] = mark

    barrier = pltpu.get_barrier_semaphore()
    for neighbour in (up, down, partner):
        pl.semaphore_signal(barrier, inc=1, device_id={"blk": neighbour})
    pl.semaphore_wait(barrier, 3)

    def slot_of(way, hop):
        return hop if way == 0 else (chips - hop) % chips

    def chunk_rows(way, hop, j, c):
        if way == 1:
            j = (j + half) % per_block
        start = slot_of(way, hop) * chip_rows + c * slots + j * CHUNK
        return pl.ds(pl.multiple_of(start, CHUNK), CHUNK)

    def send(way, k):
        hop, j = k // per_block, k % per_block
        return pltpu.make_async_remote_copy(
            src_ref=rows.at[chunk_rows(way, hop, j, core)],
            dst_ref=rows.at[chunk_rows(way, hop + 1, j, core)],
            send_sem=send_sem.at[way, k],
            recv_sem=recv_sem.at[way, k],
            device_id={"blk": up if way == 0 else down},
        )

    def push(way, k):
        hop, j = k // per_block, k % per_block
        at = rows.at[chunk_rows(way, hop + 1, j, core)]
        return pltpu.make_async_remote_copy(
            src_ref=at, dst_ref=at, send_sem=push_sem.at[way, k], recv_sem=land_sem.at[way, k],
            device_id={"blk": partner},
        )

    def mark_send_of(way, hop):
        return pltpu.make_async_remote_copy(
            src_ref=marks.at[slot_of(way, hop) * CORES + core],
            dst_ref=marks.at[slot_of(way, hop + 1) * CORES + core],
            send_sem=mark_send.at[way, hop],
            recv_sem=mark_recv.at[way, hop],
            device_id={"blk": up if way == 0 else down},
        )

    def mark_push_of(way, hop):
        at = marks.at[slot_of(way, hop) * CORES + core]
        return pltpu.make_async_remote_copy(
            src_ref=at, dst_ref=at, send_sem=mark_push.at[way, hop], recv_sem=mark_land.at[way, hop],
            device_id={"blk": partner},
        )

    own_at = rows.at[pl.ds(pl.multiple_of(core * slots, slots), slots)]
    own_push = pltpu.make_async_remote_copy(
        src_ref=own_at, dst_ref=own_at, send_sem=load_sem.at[2], recv_sem=load_sem.at[3],
        device_id={"blk": partner},
    )

    own.wait()
    for way in (0, 1):
        mark_send_of(way, 0).start()
    for k in range(per_block):
        for way in (0, 1):
            send(way, k).start()
    own_push.start()
    mark_push_of(0, 0).start()

    for t in range(npts // LANES):
        row = cover_ref[pl.ds(t, 1), :] * scale
        col = jnp.broadcast_to(row, (LANES, LANES)).T
        covb[pl.ds(t * LANES, LANES), :] = col
        best[pl.ds(t * LANES, LANES), :] = col
    resident.wait()

    def tile_work(slot, tile):
        at = pl.ds(pl.multiple_of(tile * TILE, TILE), TILE)
        block = rows[pl.ds(pl.multiple_of(slot * chip_rows, chip_rows), chip_rows), :]
        similar = lax.dot_general(
            pts[at, :], block, (((1,), (1,)), ((), ())), preferred_element_type=jnp.float32
        )
        cover = covb[at, :]
        high = best[at, :]
        for c in range(CORES):
            mine = similar[:, c * slots : (c + 1) * slots]
            over = jnp.maximum(mine - cover, 0.0)
            gacc[c] += jnp.sum(over.reshape(TILE // 8, 8, slots), axis=0)
            high = jnp.maximum(high, mine + marks[slot * CORES + c])
        best[at, :] = high

    def clear():
        gacc[...] = jnp.zeros_like(gacc)

    def store_sums(slot):
        for c in range(CORES):
            sums[slot * CORES + c] = jnp.sum(gacc[c], axis=0, keepdims=True)

    def sum_copy(slot, owner_core):
        owner = ((z + chips - slot) % chips) * CORES + owner_core
        return pltpu.make_async_remote_copy(
            src_ref=sums.at[slot * CORES + owner_core],
            dst_ref=inbox.at[slot * CORES + (core + owner_core) % CORES],
            send_sem=sum_send,
            recv_sem=sum_recv,
            device_id={"blk": owner},
        )

    def send_sums(slot):
        for c in range(CORES):
            sum_copy(slot, c).start()

    def run_tiles(slot, first, last):
        def body(tile, carry):
            tile_work(slot, tile)
            return carry

        lax.fori_loop(first, last, body, 0)

    def arrive(k, forward):
        for way in (0, 1):
            send(way, k).wait_recv()
            if forward is True:
                send(way, k + per_block).start()
            elif forward is not None:

                @pl.when(forward)
                def _():
                    send(way, k + per_block).start()

            push(way, k).start()

    def mark_arrive(hop, ways, forward_ways):
        for way in ways:
            mark_send_of(way, hop - 1).wait_recv()
            if way in forward_ways:
                mark_send_of(way, hop).start()
            mark_push_of(way, hop).start()

    def landed(hop, ways):
        for way in ways:
            for j in range(per_block):
                push(way, (hop - 1) * per_block + j).wait_recv()
            mark_push_of(way, hop).wait_recv()

    mark_arrive(1, (0, 1), (0, 1))
    own_push.wait_recv()
    mark_push_of(0, 0).wait_recv()
    clear()
    for j in range(per_block):
        run_tiles(0, j * tiles // per_block, (j + 1) * tiles // per_block)
        arrive(j, True)
    store_sums(0)

    def hop_body(hop, carry):
        for way in (0, 1):
            mark_send_of(way, hop).wait_recv()
            if way == 0:
                mark_send_of(way, hop + 1).start()
            else:

                @pl.when(hop < far - 2)
                def _():
                    mark_send_of(1, hop + 1).start()

            mark_push_of(way, hop + 1).start()
        for j in range(per_block):
            k = hop * per_block + j
            arrive(k, True if j < half else hop < far - 2)
            if j % half == 0:
                way = j // half
                landed(hop, (way,))
                clear()
            slot = slot_of(j // half, hop)
            run_tiles(slot, (j % half) * tiles // half, (j % half + 1) * tiles // half)
            if j % half == half - 1:
                store_sums(slot)
                send_sums(slot)
        return carry

    lax.fori_loop(1, far - 1, hop_body, 0)

    mark_arrive(far, (0,), ())
    for way in (0, 1):
        for j in range(way * half, way * half + half):
            if j % half == 0:
                landed(far - 1, (way,))
                clear()
            if way == 0:
                arrive((far - 1) * per_block + j, None)
            slot = slot_of(way, far - 1)
            run_tiles(slot, (j % half) * tiles // half, (j % half + 1) * tiles // half)
        store_sums(slot)
        send_sums(slot)
    for way in (0, 1):
        for j in range(half):
            push(way, (far - 1) * per_block + j).wait_recv()
    mark_push_of(0, far).wait_recv()
    clear()
    run_tiles(far, 0, tiles)
    store_sums(far)
    send_sums(far)

    sum_copy(0, 1 - core).start()
    inbox[0] = sums[core]

    for t in range(npts // LANES):
        newcov_ref[pl.ds(t, 1), :] = (
            jnp.max(best[pl.ds(t * LANES, LANES), :].T, axis=0, keepdims=True) * factor
        )

    own_push.wait_send()
    for way in (0, 1):
        for k in range(steps):
            send(way, k).wait_send()
            push(way, k).wait_send()
        for hop in range(far if way == 0 else far - 1):
            mark_send_of(way, hop).wait_send()
            mark_push_of(way, hop + 1).wait_send()
    mark_push_of(0, 0).wait_send()

    others = chips * CORES - 1
    pltpu.make_async_copy(sums.at[pl.ds(0, others)], sums.at[pl.ds(0, others)], sum_send).wait()
    pltpu.make_async_copy(inbox.at[pl.ds(1, others)], inbox.at[pl.ds(1, others)], sum_recv).wait()
    total = jnp.sum(inbox[...], axis=0)
    gain_ref[...] = jnp.where(lane < count_ref[0], total * factor / total_points, 0.0)


def per_device(points, coverage, candidates, cand_count, acc_index):
    npts, width = points.shape
    slots = candidates.shape[0]
    blocks = lax.axis_size("blk")
    chips = blocks // CORES
    per_block = slots // CHUNK
    steps = (chips // 2 - 1) * per_block + per_block // 2
    vmem = pl.BlockSpec(memory_space=pltpu.VMEM)
    smem = pl.BlockSpec(memory_space=pltpu.SMEM)
    hbm = pl.BlockSpec(memory_space=pl.ANY)
    dma = pltpu.SemaphoreType.DMA
    gain, cover = pl.pallas_call(
        functools.partial(kernel, chips, float(npts * blocks)),
        out_shape=(
            jax.ShapeDtypeStruct((1, slots), jnp.float32),
            jax.ShapeDtypeStruct((npts // LANES, LANES), jnp.float32),
        ),
        in_specs=[smem, smem, hbm, vmem, hbm],
        out_specs=(vmem, vmem),
        scratch_shapes=[
            pltpu.VMEM((npts, width), jnp.bfloat16),
            pltpu.VMEM((blocks * slots, width), jnp.bfloat16),
            pltpu.VMEM((npts, LANES), jnp.float32),
            pltpu.VMEM((npts, LANES), jnp.float32),
            pltpu.VMEM((blocks, 1, slots), jnp.float32),
            pltpu.VMEM((CORES, 8, slots), jnp.float32),
            pltpu.VMEM((blocks, 1, slots), jnp.float32),
            pltpu.VMEM((blocks, 1, slots), jnp.float32),
            dma((4,)),
            dma((2, steps)),
            dma((2, steps)),
            dma((2, steps)),
            dma((2, steps)),
            dma((2, chips // 2 + 1)),
            dma((2, chips // 2 + 1)),
            dma((2, chips // 2 + 1)),
            dma((2, chips // 2 + 1)),
            dma,
            dma,
        ],
        compiler_params=pltpu.CompilerParams(
            collective_id=0, has_side_effects=True, vmem_limit_bytes=48 * 1024 * 1024
        ),
        cost_estimate=pl.CostEstimate(
            flops=2 * npts * width * blocks * slots, bytes_accessed=npts * width * 2, transcendentals=0
        ),
    )(cand_count, acc_index, points, coverage.reshape(npts // LANES, LANES), candidates)
    return gain.reshape(slots), cover.reshape(npts)


def solution(mesh):
    return jax.shard_map(
        per_device,
        mesh=mesh,
        in_specs=(
            P(GROUPS_BLK, None),
            P(GROUPS_BLK),
            P(GROUPS_BLK, None),
            P(GROUPS_BLK),
            P(GROUPS_BLK, None),
        ),
        out_specs=(P(GROUPS_BLK), P(GROUPS_BLK)),
        check_vma=False,
    )
```

time: 138 us -> 80.2 us (0.58)
  Pallas kernels: 0 us -> 73.4 us
  waiting for transfers between devices: 49.5 us -> 0 us
  blocking collectives: 41.2 us -> 0 us
  matrix products: 20.2 us -> 0 us
  between operations: 14.8 us -> 1.3 us
  starting transfers between devices: 7.28 us -> 0 us
  local copies, waits for them, and re-layouts: 1.61 us -> 5.3 us
  other arithmetic: 2.62 us -> 0 us
    pallas_call x0 -> x1, Pallas kernels: none -> 73.4 us  [per_device(): pl.pallas_call(functools.partial(kernel, chips, float(npts * blocks)), ou...]
    all_gather x1 -> x0, blocking collectives: 41.2 us -> none  [gathered_by_axis(): nearer = lax.all_gather(shard, axes[-1], axis=dim, tiled=True)]
    all_gather x2 -> x0, waiting for transfers between devices: 40.9 us -> none  [the longest x1 40.9 us: per_device(): shard_rows = lax.all_gather(candidates, BLK, axis=0, tiled=True)]
    dot_general x2 -> x0, matrix products: 20.2 us -> none  [the longest x1 17.1 us: block_terms(): jnp.einsum('pd,cd->pc', points, cand_block, preferred_element_type=jnp.fl...]
    all_to_all x1 -> x0, waiting for transfers between devices: 7.85 us -> none  [summed_on_arrival(): lax.all_to_all(parts, axis, split_axis=0, concat_axis=0, tiled=True)]
    all_to_all x1 -> x0, starting transfers between devices: 7.16 us -> none  [summed_on_arrival(): lax.all_to_all(parts, axis, split_axis=0, concat_axis=0, tiled=True)]
    unnamed x4 -> x10, local copies, waits for them, and re-layouts: 0.01 us -> 5.3 us
    gather x1 -> x0, local copies, waits for them, and re-layouts: 1.59 us -> none  [per_device(): picked = jnp.take(candidates, acc_index[0], axis=0)]
  transfers between devices with their start and end apart: 3 -> 0, of which waited for: 2 -> 0; matrix products, arithmetic and copies ran while one was open for 17% -> 0% of each run, Pallas kernels for 0% -> 0%
where the time goes in v1:
time: 80.2 us; the launch traced here: 80 us
  Pallas kernels  73.4 us (92%)
  local copies, waits for them, and re-layouts  5.3 us (7%)
  between operations  1.3 us (2%)
    pallas_call x1, Pallas kernels, per_device(): pl.pallas_call(functools.partial(kernel, chips, float(npts * blocks)), ou...  73.4 us
    unnamed x10, local copies, waits for them, and re-layouts  5.3 us

profile of v1, /device:TPU:69, one launch (start us, length us, event | category | flops | bytes accessed | tf_op | source)
XLA Modules:
  0.0 80.0 jit_solution(11480959730869634156)
XLA Ops:
  1.3 0.0 copy-start
  1.3 1.9 %copy-done = bf16[1536,1024]{1,0:T(8,128)(2,1)S(1)} copy-done((bf16[1536,1024]{1,0:T(8,128)(2,1)S(1)}, bf16[1536,1024]{1,0:T(8,128)(2,1)}, u32[]{:S(2)}) %copy-start) | copy-done | bytes 3145752
  3.2 0.0 copy-start.1
  3.2 0.9 %copy-done.1 = bf16[128,1024]{1,0:T(8,128)(2,1)S(1)} copy-done((bf16[128,1024]{1,0:T(8,128)(2,1)S(1)}, bf16[128,1024]{1,0:T(8,128)(2,1)}, u32[]{:S(2)}) %copy-start.1) | copy-done | bytes 262168
  4.1 0.0 copy-start.2
  4.1 0.7 copy-done.2
  4.8 0.0 copy-start.3
  4.8 0.7 copy-done.3
  5.5 73.4 %shard_map.68 = (f32[1,128]{1,0:T(1,128)S(1)}, f32[12,128]{1,0:T(8,128)S(1)}) custom-call(s32[1]{0:T(128)S(6)} %copy.9.count_ref, s32[1,16]{1,0:T(1,128)S(1)} %copy-done.3, bf16[1536,1024]{1,0:T(8,128)(2,1)S(1)} %copy-done, f32[12,128]{1,0:T(8,128)S(1)} %bitcast.4, bf16[128,1024]{1,0:T(8,128)(2,1)S(1)} %copy-done.1), custom_call_target="tpu_custom_call" | custom-call | flops 12884901888 | bytes 3145728 | tf_op jit(solution)/shard_map/pallas_call | solution.py:288
  78.9 0.5 copy.10
  79.4 0.6 copy.11
Async XLA Ops:
  1.3 1.9 %copy-start = (bf16[1536,1024]{1,0:T(8,128)(2,1)S(1)}, bf16[1536,1024]{1,0:T(8,128)(2,1)}, u32[]{:S(2)}) copy-start(bf16[1536,1024]{1,0:T(8,128)(2,1)} %points_hbm.1) | copy-start | bytes 9437188
  3.2 0.9 %copy-start.1 = (bf16[128,1024]{1,0:T(8,128)(2,1)S(1)}, bf16[128,1024]{1,0:T(8,128)(2,1)}, u32[]{:S(2)}) copy-start(bf16[128,1024]{1,0:T(8,128)(2,1)} %cands_hbm.1) | copy-start | bytes 786436
  4.1 0.7 copy-start.2
  4.8 0.7 copy-start.3

commit v2 on v0

v2 whole, which is shorter than its diff:
```python
import functools

import jax
import jax.numpy as jnp
from jax import lax
from jax.experimental import pallas as pl
from jax.experimental.pallas import tpu as pltpu
from jax.sharding import PartitionSpec as P

GROUPS_BLK = ("groups", "blk")
CORES = 2
LANES = 128
TILE = 768
SHORT = 2
DEAD = -3.0e38


def kernel(
    chips, total_points, acc_hbm, points_hbm, cover_hbm, cands_hbm,
    gain_ref, newcov_ref,
    acc_ref, cover_ref, pts, rows, covb, best, marks, gacc, sums, inbox, ghost,
    load_sem, send_sem, push_sem, recv_sem, land_sem, sum_sem,
):
    npts, width = pts.shape
    slots = cands_hbm.shape[0]
    chip_rows = CORES * slots
    set_rows = slots // 2
    chunk = set_rows // 2
    short = (chips - 1) // 3
    long = 2 * short
    tiles = npts // TILE
    scale = jnp.sqrt(jnp.float32(width))
    factor = 1.0 / scale

    me = lax.axis_index("blk")
    z, core = me // CORES, me % CORES
    ahead = [((z + 1) % chips) * CORES + core, ((z + chips - 1) % chips) * CORES + core]
    partner = z * CORES + (1 - core)
    lane = lax.broadcasted_iota(jnp.int32, (1, LANES), 1)
    low = lane < set_rows

    own_at = rows.at[pl.ds(pl.multiple_of(core * slots, slots), slots)]
    accepted = pltpu.make_async_copy(acc_hbm, acc_ref, load_sem.at[0])
    own = pltpu.make_async_copy(cands_hbm, own_at, load_sem.at[1])
    covered = pltpu.make_async_copy(cover_hbm, cover_ref, load_sem.at[2])
    resident = pltpu.make_async_copy(points_hbm, pts, load_sem.at[3])
    for load in (accepted, own, covered, resident):
        load.start()

    barrier = pltpu.get_barrier_semaphore()
    for neighbour in (*ahead, partner):
        pl.semaphore_signal(barrier, inc=1, device_id={"blk": neighbour})

    accepted.wait()
    mark = jnp.full((1, LANES), DEAD, jnp.float32)
    for a in range(acc_ref.shape[1]):
        mark = jnp.where(lane == acc_ref[0, a], 0.0, mark)
    for way in (0, 1):
        marks[way * (long + 1) * CORES + core] = mark

    pl.semaphore_wait(barrier, 3)

    def slot_of(way, hop):
        return hop if way == 0 else (chips - hop) % chips

    def rows_at(way, hop, which, part, c):
        start = slot_of(way, hop) * chip_rows + c * slots + which * set_rows + part * chunk
        return rows.at[pl.ds(pl.multiple_of(start, chunk), chunk)]

    def mark_at(way, hop, c):
        return marks.at[(way * (long + 1) + hop) * CORES + c]

    def remote(src, dst, send, recv, device):
        return pltpu.make_async_remote_copy(
            src_ref=src, dst_ref=dst, send_sem=send, recv_sem=recv, device_id={"blk": device}
        )

    def where_of(way, turn, step):
        if step is SHORT:
            return turn // 2 + 1, 1 - way, turn % 2
        return turn + 1, way, step

    def send(way, turn, step):
        hop, which, part = where_of(way, turn, step)
        return remote(
            rows_at(way, hop - 1, which, part, core), rows_at(way, hop, which, part, core),
            send_sem.at[0], recv_sem.at[way, turn, step], ahead[way],
        )

    def send_mark(way, turn):
        return remote(
            mark_at(way, turn, core), mark_at(way, turn + 1, core),
            send_sem.at[1], recv_sem.at[way, turn, 0], ahead[way],
        )

    def landing(turn, step):
        return land_sem.at[long + turn // 2] if step is SHORT else land_sem.at[turn]

    def push(way, turn, step):
        hop, which, part = where_of(way, turn, step)
        at = rows_at(way, hop, which, part, core)
        return remote(at, at, push_sem.at[0], landing(turn, step), partner)

    def push_mark(way, turn):
        at = mark_at(way, turn + 1, core)
        return remote(at, at, push_sem.at[1], landing(turn, 0), partner)

    def wait_bytes(sem, count, ref=None):
        part = (ghost if ref is None else ref).at[pl.ds(0, count)]
        pltpu.make_async_copy(part, part, sem).wait()

    line = rows.shape[1] * 2 // (LANES * 4)
    own_push = [
        remote(own_at, own_at, push_sem.at[0], load_sem.at[4], partner),
        remote(mark_at(0, 0, core), mark_at(0, 0, core), push_sem.at[1], load_sem.at[4], partner),
        remote(mark_at(1, 0, core), mark_at(1, 0, core), push_sem.at[1], load_sem.at[4], partner),
    ]

    for way in (0, 1):
        send_mark(way, 0).start()
    own.wait()
    for step in (0, 1, SHORT):
        for way in (0, 1):
            send(way, 0, step).start()
    for copy in own_push:
        copy.start()

    covered.wait()
    for t in range(npts // LANES):
        row = cover_ref[pl.ds(t, 1), :] * scale
        col = jnp.broadcast_to(row, (LANES, LANES)).T
        covb[pl.ds(t * LANES, LANES), :] = col
        best[pl.ds(t * LANES, LANES), :] = col
    resident.wait()
    wait_bytes(load_sem.at[4], slots * line + 2)

    def tile_work(way, hop, tile):
        at = pl.ds(pl.multiple_of(tile * TILE, TILE), TILE)
        pieces = []
        for c in range(CORES):
            for which, path in ((0, way), (1, 1 - way)):
                start = slot_of(path, hop) * chip_rows + c * slots + which * set_rows
                pieces.append(rows[pl.ds(pl.multiple_of(start, set_rows), set_rows), :])
        similar = lax.dot_general(
            pts[at, :], jnp.concatenate(pieces, axis=0), (((1,), (1,)), ((), ())),
            preferred_element_type=jnp.float32,
        )
        cover = covb[at, :]
        high = best[at, :]
        for c in range(CORES):
            bias = jnp.where(low, mark_at(way, hop, c)[...], mark_at(1 - way, hop, c)[...])
            mine = similar[:, c * slots : (c + 1) * slots]
            over = jnp.maximum(mine - cover, 0.0)
            gacc[c] += jnp.sum(over.reshape(TILE // 8, 8, slots), axis=0)
            high = jnp.maximum(high, mine + bias)
        best[at, :] = high

    def clear():
        gacc[...] = jnp.zeros_like(gacc)

    def store_sums(way, hop):
        for c in range(CORES):
            value = jnp.sum(gacc[c], axis=0, keepdims=True)
            first = slot_of(way, hop) * CORES + c
            second = slot_of(1 - way, hop) * CORES + c
            sums[first] = jnp.where(low, value, sums[first])
            sums[second] = jnp.where(low, sums[second], value)

    def sum_copy(slot, owner_core):
        owner = ((z + chips - slot) % chips) * CORES + owner_core
        return remote(
            sums.at[slot * CORES + owner_core], inbox.at[slot * CORES + (core + owner_core) % CORES],
            sum_sem.at[0], sum_sem.at[1], owner,
        )

    def send_sums(slot):
        for c in range(CORES):
            sum_copy(slot, c).start()

    def round_body(turn, carry):
        @pl.when(turn > 0)
        def _():
            wait_bytes(land_sem.at[turn - 1], 2 * (set_rows * line + 1))

        clear()

        def half_body(step, carry):
            @pl.when(turn < long)
            def _():
                for way in (0, 1):

                    @pl.when(step == 0)
                    def _():
                        wait_bytes(recv_sem.at[way, turn, 0], chunk * line + 1)

                    @pl.when(step != 0)
                    def _():
                        wait_bytes(recv_sem.at[way, turn, 1], chunk * line)

                    @pl.when(turn + 1 < long)
                    def _():
                        @pl.when(step == 0)
                        def _():
                            send_mark(way, turn + 1).start()

                        send(way, turn + 1, step).start()

                    @pl.when(step == 0)
                    def _():
                        push_mark(way, turn).start()

                    push(way, turn, step).start()

            for tile in range(tiles // 2):
                tile_work(0, turn, step * (tiles // 2) + tile)
            return carry

        lax.fori_loop(0, 2, half_body, 0)
        store_sums(0, turn)

        @pl.when(turn > chips // 2)
        def _():
            send_sums(slot_of(0, turn))
            send_sums(slot_of(1, turn))

        @pl.when(turn == chips // 2)
        def _():
            send_sums(chips // 2)

        @pl.when(turn < long)
        def _():
            for way in (0, 1):
                wait_bytes(recv_sem.at[way, turn, SHORT], chunk * line)

                @pl.when(turn + 1 < long)
                def _():
                    send(way, turn + 1, SHORT).start()

                push(way, turn, SHORT).start()

        @pl.when((turn > 0) & (turn % 2 == 0))
        def _():
            hop = turn // 2
            wait_bytes(land_sem.at[long + hop - 1], 2 * set_rows * line)
            clear()

            def body(tile, carry):
                tile_work(1, hop, tile)
                return carry

            lax.fori_loop(0, tiles, body, 0)
            store_sums(1, hop)
            send_sums(hop)
            send_sums(chips - hop)

        return carry

    lax.fori_loop(0, long + 1, round_body, 0)

    sum_copy(0, 1 - core).start()
    inbox[0] = sums[core]

    for t in range(npts // LANES):
        newcov_ref[pl.ds(t, 1), :] = (
            jnp.max(best[pl.ds(t * LANES, LANES), :].T, axis=0, keepdims=True) * factor
        )

    wait_bytes(send_sem.at[0], 2 * 3 * long * chunk, rows)
    wait_bytes(send_sem.at[1], 2 * long)
    wait_bytes(push_sem.at[0], 2 * 3 * long * chunk + slots, rows)
    wait_bytes(push_sem.at[1], 2 * long + 2)
    others = chips * CORES - 1
    wait_bytes(sum_sem.at[0], others)
    wait_bytes(sum_sem.at[1], others)
    gain_ref[...] = jnp.sum(inbox[...], axis=0) * factor / total_points


def per_device(points, coverage, candidates, cand_count, acc_index):
    npts, width = points.shape
    slots = candidates.shape[0]
    blocks = lax.axis_size("blk")
    chips = blocks // CORES
    long = 2 * ((chips - 1) // 3)
    assert 3 * long == 2 * (chips - 1) and slots == LANES
    vmem = pl.BlockSpec(memory_space=pltpu.VMEM)
    hbm = pl.BlockSpec(memory_space=pltpu.HBM)
    dma = pltpu.SemaphoreType.DMA
    gain, cover = pl.pallas_call(
        functools.partial(kernel, chips, float(npts * blocks)),
        out_shape=(
            jax.ShapeDtypeStruct((1, slots), jnp.float32),
            jax.ShapeDtypeStruct((npts // LANES, LANES), jnp.float32),
        ),
        in_specs=[hbm] * 4,
        out_specs=(vmem, vmem),
        scratch_shapes=[
            pltpu.SMEM(acc_index.shape, jnp.int32),
            pltpu.VMEM((npts // LANES, LANES), jnp.float32),
            pltpu.VMEM((npts, width), jnp.bfloat16),
            pltpu.VMEM((blocks * slots, width), jnp.bfloat16),
            pltpu.VMEM((npts, LANES), jnp.float32),
            pltpu.VMEM((npts, LANES), jnp.float32),
            pltpu.VMEM((2 * (long + 1) * CORES, 1, slots), jnp.float32),
            pltpu.VMEM((CORES, 8, slots), jnp.float32),
            pltpu.VMEM((blocks, 1, slots), jnp.float32),
            pltpu.VMEM((blocks, 1, slots), jnp.float32),
            pltpu.VMEM((slots * 4 + 2, 1, LANES), jnp.float32),
            dma((5,)),
            dma((2,)),
            dma((2,)),
            dma((2, long, 3)),
            dma((3 * long // 2,)),
            dma((2,)),
        ],
        compiler_params=pltpu.CompilerParams(
            collective_id=0, has_side_effects=True, vmem_limit_bytes=48 * 1024 * 1024
        ),
        cost_estimate=pl.CostEstimate(
            flops=2 * npts * width * blocks * slots, bytes_accessed=npts * width * 2, transcendentals=0
        ),
    )(*(pltpu.with_memory_space_constraint(x, pltpu.HBM) for x in (acc_index, points, coverage.reshape(npts // LANES, LANES), candidates)))
    live = jnp.arange(slots, dtype=jnp.int32) < cand_count[0]
    return jnp.where(live, gain.reshape(slots), 0.0), cover.reshape(npts)


def solution(mesh):
    return jax.shard_map(
        per_device,
        mesh=mesh,
        in_specs=(
            P(GROUPS_BLK, None),
            P(GROUPS_BLK),
            P(GROUPS_BLK, None),
            P(GROUPS_BLK),
            P(GROUPS_BLK, None),
        ),
        out_specs=(P(GROUPS_BLK), P(GROUPS_BLK)),
        check_vma=False,
    )
```

time: 138 us -> 69.5 us (0.50)
  Pallas kernels: 0 us -> 67 us
  waiting for transfers between devices: 49.5 us -> 0 us
  blocking collectives: 41.2 us -> 0 us
  matrix products: 20.2 us -> 0 us
  between operations: 14.8 us -> 1.29 us
  starting transfers between devices: 7.28 us -> 0 us
  other arithmetic: 2.62 us -> 0.51 us
    pallas_call x0 -> x1, Pallas kernels: none -> 67 us  [per_device(): pl.pallas_call(functools.partial(kernel, chips, float(npts * blocks)), ou...]
    all_gather x1 -> x0, blocking collectives: 41.2 us -> none  [gathered_by_axis(): nearer = lax.all_gather(shard, axes[-1], axis=dim, tiled=True)]
    all_gather x2 -> x0, waiting for transfers between devices: 40.9 us -> none  [the longest x1 40.9 us: per_device(): shard_rows = lax.all_gather(candidates, BLK, axis=0, tiled=True)]
    dot_general x2 -> x0, matrix products: 20.2 us -> none  [the longest x1 17.1 us: block_terms(): jnp.einsum('pd,cd->pc', points, cand_block, preferred_element_type=jnp.fl...]
    all_to_all x1 -> x0, waiting for transfers between devices: 7.85 us -> none  [summed_on_arrival(): lax.all_to_all(parts, axis, split_axis=0, concat_axis=0, tiled=True)]
    all_to_all x1 -> x0, starting transfers between devices: 7.16 us -> none  [summed_on_arrival(): lax.all_to_all(parts, axis, split_axis=0, concat_axis=0, tiled=True)]
    gather x1 -> x0, local copies, waits for them, and re-layouts: 1.59 us -> none  [per_device(): picked = jnp.take(candidates, acc_index[0], axis=0)]
  transfers between devices with their start and end apart: 3 -> 0, of which waited for: 2 -> 0; matrix products, arithmetic and copies ran while one was open for 17% -> 0% of each run, Pallas kernels for 0% -> 0%
where the time goes in v2:
time: 69.5 us; the launch traced here: 69.4 us
  Pallas kernels  67 us (96%)
  between operations  1.29 us (2%)
    pallas_call x1, Pallas kernels, per_device(): pl.pallas_call(functools.partial(kernel, chips, float(npts * blocks)), ou...  67 us

profile of v2, /device:TPU:69, one launch (start us, length us, event | category | flops | bytes accessed | tf_op | source)
XLA Modules:
  0.0 69.4 jit_solution(2575838213464991998)
XLA Ops:
  1.3 67.0 %shard_map.68 = (f32[1,128]{1,0:T(1,128)S(1)}, f32[12,128]{1,0:T(8,128)S(1)}) custom-call(s32[1,16]{1,0:T(1,128)} %acc_hbm.1, bf16[1536,1024]{1,0:T(8,128)(2,1)} %points_hbm.1, f32[12,128]{1,0:T(8,128)} %bitcast.7, bf16[128,1024]{1,0:T(8,128)(2,1)} %cands_hbm.1), custom_call_target="tpu_custom_call" | custom-call | flops 12884901888 | bytes 3145728 | tf_op jit(solution)/shard_map/pallas_call | solution.py:288
  68.3 0.5 compare_select_fusion
  68.8 0.6 copy.9

commit v3 on v2

--- a/solution.py
+++ b/solution.py
@@ -211,6 +211,12 @@
 
                     push(way, turn, step).start()
 
+            @pl.when((turn == long) & (step != 0))
+            def _():
+                for way in (0, 1):
+                    wait_bytes(recv_sem.at[way, long - 1, SHORT], chunk * line)
+                    push(way, long - 1, SHORT).start()
+
             for tile in range(tiles // 2):
                 tile_work(0, turn, step * (tiles // 2) + tile)
             return carry
@@ -227,15 +233,11 @@
         def _():
             send_sums(chips // 2)
 
-        @pl.when(turn < long)
+        @pl.when(turn + 1 < long)
         def _():
             for way in (0, 1):
                 wait_bytes(recv_sem.at[way, turn, SHORT], chunk * line)
-
-                @pl.when(turn + 1 < long)
-                def _():
-                    send(way, turn + 1, SHORT).start()
-
+                send(way, turn + 1, SHORT).start()
                 push(way, turn, SHORT).start()
 
         @pl.when((turn > 0) & (turn % 2 == 0))
@@ -260,10 +262,14 @@
     sum_copy(0, 1 - core).start()
     inbox[0] = sums[core]
 
-    for t in range(npts // LANES):
-        newcov_ref[pl.ds(t, 1), :] = (
-            jnp.max(best[pl.ds(t * LANES, LANES), :].T, axis=0, keepdims=True) * factor
-        )
+    def cover_body(block, carry):
+        for nth in range(4):
+            t = block * 4 + nth
+            at = pl.ds(pl.multiple_of(t * LANES, LANES), LANES)
+            newcov_ref[pl.ds(t, 1), :] = jnp.max(best[at, :].T, axis=0, keepdims=True) * factor
+        return carry
+
+    lax.fori_loop(0, npts // LANES // 4, cover_body, 0)
 
     wait_bytes(send_sem.at[0], 2 * 3 * long * chunk, rows)
     wait_bytes(send_sem.at[1], 2 * long)

time: 69.5 us -> 69.9 us (level)
  no operation moved by 1% of the time
where the time goes in v3:
time: 69.9 us; the launch traced here: 69.8 us
  Pallas kernels  67.4 us (96%)
  between operations  1.29 us (2%)
    pallas_call x1, Pallas kernels, per_device(): pl.pallas_call(functools.partial(kernel, chips, float(npts * blocks)), ou...  67.4 us

profile of v3, /device:TPU:69, one launch (start us, length us, event | category | flops | bytes accessed | tf_op | source)
XLA Modules:
  0.0 69.8 jit_solution(3055132150727961969)
XLA Ops:
  1.3 67.4 %shard_map.68 = (f32[1,128]{1,0:T(1,128)S(1)}, f32[12,128]{1,0:T(8,128)S(1)}) custom-call(s32[1,16]{1,0:T(1,128)} %acc_hbm.1, bf16[1536,1024]{1,0:T(8,128)(2,1)} %points_hbm.1, f32[12,128]{1,0:T(8,128)} %bitcast.7, bf16[128,1024]{1,0:T(8,128)(2,1)} %cands_hbm.1), custom_call_target="tpu_custom_call" | custom-call | flops 12884901888 | bytes 3145728 | tf_op jit(solution)/shard_map/pallas_call | solution.py:294
  68.7 0.5 compare_select_fusion
  69.2 0.6 copy.9

commit v4 on v2

v4 whole, which is shorter than its diff:
```python
import functools

import jax
import jax.numpy as jnp
from jax import lax
from jax.experimental import pallas as pl
from jax.experimental.pallas import tpu as pltpu
from jax.sharding import PartitionSpec as P

GROUPS_BLK = ("groups", "blk")
CORES = 2
LANES = 128
TILE = 768
PARTS = 4
DEAD = -3.0e38


def kernel(
    chips, total_points, acc_hbm, points_hbm, cover_hbm, cands_hbm,
    gain_ref, newcov_ref,
    acc_ref, cover_ref, pts, rows, covb, best, marks, gacc, sums, inbox, ghost,
    load_sem, send_sem, push_sem, recv_sem, land_sem, sum_sem,
):
    npts, width = pts.shape
    slots = cands_hbm.shape[0]
    chip_rows = CORES * slots
    chunk = slots // PARTS
    far = chips // 2
    tiles = npts // TILE
    scale = jnp.sqrt(jnp.float32(width))
    factor = 1.0 / scale

    me = lax.axis_index("blk")
    z, core = me // CORES, me % CORES
    ahead = [((z + 1) % chips) * CORES + core, ((z + chips - 1) % chips) * CORES + core]
    partner = z * CORES + (1 - core)
    lane = lax.broadcasted_iota(jnp.int32, (1, LANES), 1)

    own_at = rows.at[pl.ds(pl.multiple_of(core * slots, slots), slots)]
    accepted = pltpu.make_async_copy(acc_hbm, acc_ref, load_sem.at[0])
    own = pltpu.make_async_copy(cands_hbm, own_at, load_sem.at[1])
    covered = pltpu.make_async_copy(cover_hbm, cover_ref, load_sem.at[2])
    resident = pltpu.make_async_copy(points_hbm, pts, load_sem.at[3])
    for load in (accepted, own, covered, resident):
        load.start()

    barrier = pltpu.get_barrier_semaphore()
    for neighbour in (*ahead, partner):
        pl.semaphore_signal(barrier, inc=1, device_id={"blk": neighbour})

    accepted.wait()
    mark = jnp.full((1, LANES), DEAD, jnp.float32)
    for a in range(acc_ref.shape[1]):
        mark = jnp.where(lane == acc_ref[0, a], 0.0, mark)
    marks[core] = mark

    pl.semaphore_wait(barrier, 3)

    def slot_of(way, hop):
        return hop if way == 0 else (chips - hop) % chips

    def rows_at(way, hop, part):
        nth = part if way == 0 else (part + PARTS // 2) % PARTS
        start = slot_of(way, hop) * chip_rows + core * slots + nth * chunk
        return rows.at[pl.ds(pl.multiple_of(start, chunk), chunk)]

    def mark_at(way, hop, c):
        return marks.at[slot_of(way, hop) * CORES + c]

    def remote(src, dst, send, recv, device):
        return pltpu.make_async_remote_copy(
            src_ref=src, dst_ref=dst, send_sem=send, recv_sem=recv, device_id={"blk": device}
        )

    def send(way, turn, part):
        return remote(
            rows_at(way, turn, part), rows_at(way, turn + 1, part),
            send_sem.at[0], recv_sem.at[way, turn, part], ahead[way],
        )

    def send_mark(way, turn):
        return remote(
            mark_at(way, turn, core), mark_at(way, turn + 1, core),
            send_sem.at[1], recv_sem.at[way, turn, 0], ahead[way],
        )

    def push(way, turn, part):
        at = rows_at(way, turn + 1, part)
        return remote(at, at, push_sem.at[0], land_sem.at[turn], partner)

    def push_mark(way, turn):
        at = mark_at(way, turn + 1, core)
        return remote(at, at, push_sem.at[1], land_sem.at[turn], partner)

    def wait_bytes(sem, count, ref=None):
        part = (ghost if ref is None else ref).at[pl.ds(0, count)]
        pltpu.make_async_copy(part, part, sem).wait()

    line = rows.shape[1] * 2 // (LANES * 4)
    own_push = [
        remote(own_at, own_at, push_sem.at[0], load_sem.at[4], partner),
        remote(mark_at(0, 0, core), mark_at(0, 0, core), push_sem.at[1], load_sem.at[4], partner),
    ]

    for way in (0, 1):
        send_mark(way, 0).start()
    own.wait()
    for part in range(PARTS):
        for way in (0, 1):
            send(way, 0, part).start()
    for copy in own_push:
        copy.start()

    covered.wait()
    for t in range(npts // LANES):
        row = cover_ref[pl.ds(t, 1), :] * scale
        col = jnp.broadcast_to(row, (LANES, LANES)).T
        covb[pl.ds(t * LANES, LANES), :] = col
        best[pl.ds(t * LANES, LANES), :] = col
    resident.wait()
    wait_bytes(load_sem.at[4], slots * line + 1)

    def tile_work(slot, tile):
        at = pl.ds(pl.multiple_of(tile * TILE, TILE), TILE)
        block = rows[pl.ds(pl.multiple_of(slot * chip_rows, chip_rows), chip_rows), :]
        similar = lax.dot_general(
            pts[at, :], block, (((1,), (1,)), ((), ())), preferred_element_type=jnp.float32
        )
        cover = covb[at, :]
        high = best[at, :]
        for c in range(CORES):
            mine = similar[:, c * slots : (c + 1) * slots]
            over = jnp.maximum(mine - cover, 0.0)
            gacc[c] += jnp.sum(over.reshape(TILE // 8, 8, slots), axis=0)
            high = jnp.maximum(high, mine + marks[slot * CORES + c])
        best[at, :] = high

    def sum_copy(slot, owner_core):
        owner = ((z + chips - slot) % chips) * CORES + owner_core
        return remote(
            sums.at[slot * CORES + owner_core], inbox.at[slot * CORES + (core + owner_core) % CORES],
            sum_sem.at[0], sum_sem.at[1], owner,
        )

    def send_sums(slot):
        for c in range(CORES):
            sum_copy(slot, c).start()

    def arrive(turn, part):
        for way in (0, 1):

            @pl.when((part == 0) & (turn < far - way))
            def _():
                wait_bytes(recv_sem.at[way, turn, 0], chunk * line + 1)

            @pl.when((part != 0) | (turn == far - way))
            def _():
                wait_bytes(recv_sem.at[way, turn, part], chunk * line)

            @pl.when((part == 0) & (turn + 1 < far - way))
            def _():
                send_mark(way, turn + 1).start()

            @pl.when((turn + 2 < far) | ((turn + 2 == far) & (part < PARTS // 2)))
            def _():
                send(way, turn + 1, part).start()

            @pl.when((part == 0) & (turn < far - way))
            def _():
                push_mark(way, turn).start()

            push(way, turn, part).start()

    def round_body(turn, carry):
        @pl.when((turn > 0) & (turn < far))
        def _():
            wait_bytes(land_sem.at[turn - 1], 2 * (slots * line + 1))

        @pl.when(turn == far)
        def _():
            wait_bytes(land_sem.at[turn - 1], slots * line + 1)

        def step_body(step, carry):
            way, tile = step // 2, step % 2
            slot = jnp.where(way == 0, turn, chips - turn)

            @pl.when(turn < far - 1)
            def _():
                arrive(turn, step)

            @pl.when((way == 0) | ((turn > 0) & (turn < far)))
            def _():
                @pl.when(tile == 0)
                def _():
                    gacc[...] = jnp.zeros_like(gacc)

                tile_work(slot, tile)

            @pl.when((turn == far - 1) & (tile == 0))
            def _():
                arrive(turn, way)

            @pl.when((tile == 1) & ((way == 0) | ((turn > 0) & (turn < far))))
            def _():
                for c in range(CORES):
                    sums[slot * CORES + c] = jnp.sum(gacc[c], axis=0, keepdims=True)

                @pl.when(turn > 0)
                def _():
                    send_sums(slot)

            return carry

        lax.fori_loop(0, jnp.where(turn == far, 2, PARTS), step_body, 0)
        return carry

    lax.fori_loop(0, far + 1, round_body, 0)

    sum_copy(0, 1 - core).start()
    inbox[0] = sums[core]

    for t in range(npts // LANES):
        newcov_ref[pl.ds(t, 1), :] = (
            jnp.max(best[pl.ds(t * LANES, LANES), :].T, axis=0, keepdims=True) * factor
        )

    moved = (chips - 1) * slots
    wait_bytes(send_sem.at[0], moved, rows)
    wait_bytes(send_sem.at[1], chips - 1)
    wait_bytes(push_sem.at[0], moved + slots, rows)
    wait_bytes(push_sem.at[1], chips)
    others = chips * CORES - 1
    wait_bytes(sum_sem.at[0], others)
    wait_bytes(sum_sem.at[1], others)
    gain_ref[...] = jnp.sum(inbox[...], axis=0) * factor / total_points


def per_device(points, coverage, candidates, cand_count, acc_index):
    npts, width = points.shape
    slots = candidates.shape[0]
    blocks = lax.axis_size("blk")
    chips = blocks // CORES
    far = chips // 2
    assert npts == 2 * TILE and slots == LANES
    vmem = pl.BlockSpec(memory_space=pltpu.VMEM)
    hbm = pl.BlockSpec(memory_space=pltpu.HBM)
    dma = pltpu.SemaphoreType.DMA
    gain, cover = pl.pallas_call(
        functools.partial(kernel, chips, float(npts * blocks)),
        out_shape=(
            jax.ShapeDtypeStruct((1, slots), jnp.float32),
            jax.ShapeDtypeStruct((npts // LANES, LANES), jnp.float32),
        ),
        in_specs=[hbm] * 4,
        out_specs=(vmem, vmem),
        scratch_shapes=[
            pltpu.SMEM(acc_index.shape, jnp.int32),
            pltpu.VMEM((npts // LANES, LANES), jnp.float32),
            pltpu.VMEM((npts, width), jnp.bfloat16),
            pltpu.VMEM((blocks * slots, width), jnp.bfloat16),
            pltpu.VMEM((npts, LANES), jnp.float32),
            pltpu.VMEM((npts, LANES), jnp.float32),
            pltpu.VMEM((blocks, 1, slots), jnp.float32),
            pltpu.VMEM((CORES, 8, slots), jnp.float32),
            pltpu.VMEM((blocks, 1, slots), jnp.float32),
            pltpu.VMEM((blocks, 1, slots), jnp.float32),
            pltpu.VMEM((slots * 8 + 2, 1, LANES), jnp.float32),
            dma((5,)),
            dma((2,)),
            dma((2,)),
            dma((2, far, PARTS)),
            dma((far,)),
            dma((2,)),
        ],
        compiler_params=pltpu.CompilerParams(
            collective_id=0, has_side_effects=True, vmem_limit_bytes=48 * 1024 * 1024
        ),
        cost_estimate=pl.CostEstimate(
            flops=2 * npts * width * blocks * slots, bytes_accessed=npts * width * 2, transcendentals=0
        ),
    )(*(pltpu.with_memory_space_constraint(x, pltpu.HBM) for x in (acc_index, points, coverage.reshape(npts // LANES, LANES), candidates)))
    live = jnp.arange(slots, dtype=jnp.int32) < cand_count[0]
    return jnp.where(live, gain.reshape(slots), 0.0), cover.reshape(npts)


def solution(mesh):
    return jax.shard_map(
        per_device,
        mesh=mesh,
        in_specs=(
            P(GROUPS_BLK, None),
            P(GROUPS_BLK),
            P(GROUPS_BLK, None),
            P(GROUPS_BLK),
            P(GROUPS_BLK, None),
        ),
        out_specs=(P(GROUPS_BLK), P(GROUPS_BLK)),
        check_vma=False,
    )
```

time: 69.5 us -> 71.3 us (1.026)
  Pallas kernels: 67 us -> 68.8 us
    pallas_call x1, Pallas kernels: 67 us -> 68.8 us  [per_device(): pl.pallas_call(functools.partial(kernel, chips, float(npts * blocks)), ou...]
where the time goes in v4:
time: 71.3 us; the launch traced here: 71.2 us
  Pallas kernels  68.8 us (96%)
  between operations  1.29 us (2%)
    pallas_call x1, Pallas kernels, per_device(): pl.pallas_call(functools.partial(kernel, chips, float(npts * blocks)), ou...  68.8 us

profile of v4, /device:TPU:69, one launch (start us, length us, event | category | flops | bytes accessed | tf_op | source)
XLA Modules:
  0.0 71.2 jit_solution(10474553666749971698)
XLA Ops:
  1.3 68.8 %shard_map.68 = (f32[1,128]{1,0:T(1,128)S(1)}, f32[12,128]{1,0:T(8,128)S(1)}) custom-call(s32[1,16]{1,0:T(1,128)} %acc_hbm.1, bf16[1536,1024]{1,0:T(8,128)(2,1)} %points_hbm.1, f32[12,128]{1,0:T(8,128)} %bitcast.7, bf16[128,1024]{1,0:T(8,128)(2,1)} %cands_hbm.1), custom_call_target="tpu_custom_call" | custom-call | flops 12884901888 | bytes 3145728 | tf_op jit(solution)/shard_map/pallas_call | solution.py:248
  70.0 0.5 compare_select_fusion
  70.6 0.6 copy.9

commit v5 on v3

--- a/solution.py
+++ b/solution.py
@@ -279,6 +279,34 @@
     wait_bytes(sum_sem.at[0], others)
     wait_bytes(sum_sem.at[1], others)
     gain_ref[...] = jnp.sum(inbox[...], axis=0) * factor / total_points
+
+
+def finish(count_ref, gain_ref, cover_ref, gain_hbm, cover_hbm, live_ref, sems):
+    covered = pltpu.make_async_copy(cover_ref, cover_hbm, sems.at[0])
+    covered.start()
+    lane = lax.broadcasted_iota(jnp.int32, gain_ref.shape, 1)
+    live_ref[...] = jnp.where(lane < count_ref[0], gain_ref[...], 0.0)
+    gained = pltpu.make_async_copy(live_ref, gain_hbm, sems.at[1])
+    gained.start()
+    covered.wait()
+    gained.wait()
+
+
+def finished(count, gain, cover):
+    vmem = pl.BlockSpec(memory_space=pltpu.VMEM)
+    hbm = pl.BlockSpec(memory_space=pltpu.HBM)
+    gain_out, cover_out = pl.pallas_call(
+        finish,
+        out_shape=(
+            jax.ShapeDtypeStruct(gain.shape, gain.dtype),
+            jax.ShapeDtypeStruct(cover.shape, cover.dtype),
+        ),
+        in_specs=[pl.BlockSpec(memory_space=pltpu.SMEM), vmem, vmem],
+        out_specs=(hbm, hbm),
+        scratch_shapes=[pltpu.VMEM(gain.shape, gain.dtype), pltpu.SemaphoreType.DMA((2,))],
+        compiler_params=pltpu.CompilerParams(vmem_limit_bytes=1024 * 1024),
+    )(count, gain, cover)
+    return gain_out.reshape(gain.size), cover_out.reshape(cover.size)
 
 
 def per_device(points, coverage, candidates, cand_count, acc_index):
@@ -325,8 +353,7 @@
             flops=2 * npts * width * blocks * slots, bytes_accessed=npts * width * 2, transcendentals=0
         ),
     )(*(pltpu.with_memory_space_constraint(x, pltpu.HBM) for x in (acc_index, points, coverage.reshape(npts // LANES, LANES), candidates)))
-    live = jnp.arange(slots, dtype=jnp.int32) < cand_count[0]
-    return jnp.where(live, gain.reshape(slots), 0.0), cover.reshape(npts)
+    return finished(cand_count, gain, cover)
 
 
 def solution(mesh):

time: 69.9 us -> 69.4 us (level)
  no operation moved by 1% of the time
where the time goes in v5:
time: 69.4 us; the launch traced here: 69.3 us
  Pallas kernels  68 us (98%)
  between operations  1.29 us (2%)
    pallas_call x1, Pallas kernels, per_device(): pl.pallas_call(functools.partial(kernel, chips, float(npts * blocks)), ou...  67.4 us

profile of v5, /device:TPU:69, one launch (start us, length us, event | category | flops | bytes accessed | tf_op | source)
XLA Modules:
  0.0 69.3 jit_solution(16539759304906846374)
XLA Ops:
  1.3 67.4 %shard_map.68 = (f32[1,128]{1,0:T(1,128)S(1)}, f32[12,128]{1,0:T(8,128)S(1)}) custom-call(s32[1,16]{1,0:T(1,128)} %acc_hbm.1, bf16[1536,1024]{1,0:T(8,128)(2,1)} %points_hbm.1, f32[12,128]{1,0:T(8,128)} %bitcast.3, bf16[128,1024]{1,0:T(8,128)(2,1)} %cands_hbm.1), custom_call_target="tpu_custom_call" | custom-call | flops 12884901888 | bytes 3145728 | tf_op jit(solution)/shard_map/pallas_call | solution.py:322
  68.7 0.6 shard_map.69
